TPU v7x, 32 devices: a whole 2x2x4 slice. The times are simulated.
32 devices in a mesh: expert: 16 (over z, y, x), dp: 2 (over core).
Axes of the slice: x: 2, y: 2, z: 4, core: 2. Of those that a mesh axis runs over, the one named last changes fastest.
Arguments:
- tokens: bfloat16 [4096, 1440], P(('expert', 'dp')), may hold values from -6 to 6
- cotangent: bfloat16 [4096, 1440], P(('expert', 'dp')), may hold values from -0.3984375 to 0.3984375
- expert_ids: int32 [4096, 4], P(('expert', 'dp')), may hold values from 0 to 15, all different within a row; in each aligned block of 128 rows (0 to 127, 128 to 255, ...) at most 48 rows name the same one
- gate_weights: float32 [4096, 4], P(('expert', 'dp')), may hold values from 0.05 to 1
- w_gate: bfloat16 [16, 1440, 1440], P('expert', 'dp'), may hold values from -0.15625 to 0.15625
- w_up: bfloat16 [16, 1440, 1440], P('expert', 'dp'), may hold values from -0.15625 to 0.15625
- w_down: bfloat16 [16, 1440, 1440], P('expert', 'dp'), may hold values from -0.15625 to 0.15625
Outputs:
- mixed: bfloat16 [4096, 1440], P(('expert', 'dp'))
- grad_gate: bfloat16 [16, 1440, 1440], P('expert', 'dp')
- grad_up: bfloat16 [16, 1440, 1440], P('expert', 'dp')
- grad_down: bfloat16 [16, 1440, 1440], P('expert', 'dp')
Inputs may be any that keep to these rules, and one draw needn't show every extreme that they name: `expert_ids`: each row names 4 different experts. Within the rows of one device no expert is named more than 48 times, a bound that some block reaches.
All inputs are finite; a program needn't handle non-finite values.
Results may differ from a plain program's by a relative error of at most 0.013.
Values may be sent and summed in bfloat16 or wider, within the bound.
A program may use at most 128 MiB of HBM per device.

v0:
```python
import functools

import jax
import jax.numpy as jnp
from jax import lax
from jax.experimental import pallas as pl
from jax.experimental.pallas import tpu as pltpu
from jax.sharding import PartitionSpec as P

CAP = 512
INNER = 4
SWISH_SLOPE = 1.702
F32 = jnp.float32
BF16 = jnp.bfloat16


def dot(a, b):
    return jnp.dot(a, b, preferred_element_type=F32)


def dot_nt(a, b):
    return lax.dot_general(a, b, (((1,), (1,)), ((), ())), preferred_element_type=F32)


def dot_tn(a, b):
    return lax.dot_general(a, b, (((0,), (0,)), ((), ())), preferred_element_type=F32)


def share_kernel(size, x_ref, all_ref, send_sem, recv_sem):
    me = lax.axis_index("expert")
    barrier = pltpu.get_barrier_semaphore()
    for k in range(1, size):
        pl.semaphore_signal(
            barrier, inc=1, device_id={"expert": lax.rem(me + k, size)},
            device_id_type=pl.DeviceIdType.MESH,
        )
    pl.semaphore_wait(barrier, size - 1)
    copies = []
    for k in range(1, size):
        copy = pltpu.make_async_remote_copy(
            src_ref=x_ref, dst_ref=all_ref.at[me],
            send_sem=send_sem.at[k], recv_sem=recv_sem.at[k],
            device_id={"expert": lax.rem(me + k, size)},
            device_id_type=pl.DeviceIdType.MESH,
        )
        copy.start()
        copies.append(copy)
    all_ref[me] = x_ref[...]
    for copy in copies:
        copy.wait()


def share(x):
    size = lax.axis_size("expert")
    return pl.pallas_call(
        functools.partial(share_kernel, size),
        out_shape=jax.ShapeDtypeStruct((size,) + x.shape, x.dtype),
        in_specs=[pl.BlockSpec(memory_space=pltpu.VMEM)],
        out_specs=pl.BlockSpec(memory_space=pltpu.VMEM),
        scratch_shapes=[
            pltpu.SemaphoreType.DMA((size,)),
            pltpu.SemaphoreType.DMA((size,)),
        ],
        compiler_params=pltpu.CompilerParams(collective_id=0, has_side_effects=True),
    )(x)


def body(tokens, cotangent, expert_ids, gate_weights, w_gate, w_up, w_down):
    size = lax.axis_size("expert")
    rows, top = expert_ids.shape
    width = tokens.shape[1]
    slot = 3 * rows * top // (2 * size)
    inner = min(INNER, size)
    outer = size // inner
    me = lax.axis_index("expert")
    mine_out, mine_in = me // inner, me % inner
    half = outer // 2
    partner = jnp.bitwise_xor(mine_in, jnp.arange(inner, dtype=jnp.int32))

    def shift(x, by):
        pairs = [(d, (d // inner + by) % outer * inner + d % inner) for d in range(size)]
        return lax.ppermute(x, "expert", pairs)

    def gather_outer(x):
        blocks = [x] + [None] * (outer - 1)
        for r in range(1, half + 1):
            if outer > 1:
                blocks[r] = shift(blocks[r - 1], 1)
        for r in range(1, outer - half):
            blocks[outer - r] = shift(blocks[(outer - r + 1) % outer], -1)
        return blocks

    def exchange(blocks):
        moved = list(blocks)
        for d in range(inner - 1, 0, -1):
            pairs = [(e, e // inner * inner + (e % inner ^ d)) for e in range(size)]
            moved[d] = lax.ppermute(blocks[d], "expert", pairs)
        return jnp.concatenate(moved)

    def relay(blocks):
        held = jnp.concatenate(blocks)
        return exchange([dot(part, held).astype(BF16) for part in select])

    meta = jnp.concatenate([expert_ids.T.astype(F32), gate_weights.T], axis=0)
    meta_all = share(meta)
    meta_all, tokens = lax.optimization_barrier((meta_all, tokens))
    token_blocks = gather_outer(tokens)
    token_blocks, cotangent = lax.optimization_barrier((token_blocks, cotangent))
    cot_blocks = gather_outer(cotangent)

    ids_all = meta_all[:, :top, :].astype(jnp.int32)
    gates_all = meta_all[:, top:, :]
    back = (mine_out - jnp.arange(outer, dtype=jnp.int32)) % outer

    before = (jnp.arange(rows)[:, None] < jnp.arange(rows)[None, :]).astype(BF16)

    ids_relay = jnp.stack([
        lax.dynamic_index_in_dim(ids_all, back[r] * inner + mine_in, 0, keepdims=False)
        for r in range(outer)
    ])
    near = mine_out * inner + partner
    named = jnp.any(ids_relay[None] == near[:, None, None, None], axis=2)
    rank = dot(named.astype(BF16).reshape(inner * outer, rows), before)
    rank = rank.reshape(inner, outer, rows).astype(jnp.int32)
    place = jnp.where(named, rank, slot)
    hit = place[:, :, None, :] == jnp.arange(slot, dtype=jnp.int32)[None, None, :, None]
    same = jnp.eye(outer, dtype=jnp.bool_)
    select = (hit[:, :, :, None, :] & same[None, :, None, :, None]).astype(BF16)
    select = select.reshape(inner, outer * slot, outer * rows)

    mask = jnp.any(ids_all == me, axis=1)
    gate_of = jnp.sum(jnp.where(ids_all == me, gates_all, 0.0), axis=1)
    counts = jnp.sum(mask.astype(jnp.int32), axis=1)
    below = jnp.arange(size)[:, None] > jnp.arange(size)[None, :]
    starts = jnp.sum(jnp.where(below, counts[None, :], 0), axis=1)
    own_rank = dot(mask.astype(BF16), before).astype(jnp.int32)
    position = jnp.where(mask, starts[:, None] + own_rank, CAP).reshape(1, size * rows)
    row_index = jnp.arange(CAP, dtype=jnp.int32)
    row_gate = jnp.sum(
        jnp.where(position == row_index[:, None], gate_of.reshape(1, size * rows), 0.0),
        axis=1, keepdims=True,
    )
    source = back[None, :] * inner + partner[:, None]
    is_source = source[:, :, None] == jnp.arange(size, dtype=jnp.int32)
    slot_start = jnp.sum(jnp.where(is_source, starts, 0), axis=2)
    slot_live = jnp.sum(jnp.where(is_source, counts, 0), axis=2)
    within = jnp.arange(slot, dtype=jnp.int32)
    slot_row = jnp.where(
        within < slot_live[:, :, None], slot_start[:, :, None] + within, CAP
    ).reshape(1, inner * outer * slot)
    pack = (row_index[:, None] == slot_row).astype(BF16)

    full_gate, full_up, full_down = (
        lax.all_gather(w_gate, "dp", axis=1, tiled=True)[0],
        lax.all_gather(w_up, "dp", axis=1, tiled=True)[0],
        lax.all_gather(w_down, "dp", axis=1, tiled=True)[0],
    )

    recv_x = relay(token_blocks)
    packed_x = dot(pack, recv_x).astype(BF16)
    pre_gate = dot(packed_x, full_gate)
    pre_up = dot(packed_x, full_up)
    sig = jax.nn.sigmoid(SWISH_SLOPE * pre_gate)
    value = pre_gate * sig
    slope = sig + SWISH_SLOPE * pre_gate * sig * (1.0 - sig)
    hidden = (value * (pre_up + 1.0)).astype(BF16)
    out = (dot_nt(hidden, full_down) * row_gate).astype(BF16)
    spread = dot_tn(pack, out).astype(BF16).reshape(inner, outer * slot, width)

    recv_g = relay(cot_blocks)
    spread, recv_g = lax.optimization_barrier((spread, recv_g))
    returned = exchange([spread[d] for d in range(inner)])
    packed_g = (dot(pack, recv_g) * row_gate).astype(BF16)
    grad_down = dot_tn(packed_g, hidden).astype(BF16)
    d_hidden = dot(packed_g, full_down)
    d_gate = (d_hidden * (pre_up + 1.0) * slope).astype(BF16)
    d_up = (d_hidden * value).astype(BF16)
    returned, grad_down, d_gate, d_up = lax.optimization_barrier(
        (returned, grad_down, d_gate, d_up)
    )
    partial = dot_tn(select.reshape(inner * outer * slot, outer * rows), returned)
    partial = partial.reshape(outer, rows, width)
    partial, d_gate, d_up = lax.optimization_barrier((partial, d_gate, d_up))
    grad_gate = dot_tn(packed_x, d_gate).astype(BF16)
    grad_up = dot_tn(packed_x, d_up).astype(BF16)

    total = partial[0]
    ahead = partial[half]
    behind = partial[half + 1] if outer - half > 1 else None
    for r in range(half - 1, -1, -1):
        ahead = shift(ahead.astype(BF16), -1).astype(F32)
        if r > 0:
            ahead = ahead + partial[r]
    for r in range(half + 2, outer + 1):
        behind = shift(behind.astype(BF16), 1).astype(F32)
        if r < outer:
            behind = behind + partial[r]
    if half > 0:
        total = total + ahead
    if behind is not None:
        total = total + behind
    mixed = total.astype(BF16)

    grads = [
        lax.psum_scatter(g, "dp", scatter_dimension=0, tiled=True)[None]
        for g in (grad_down, grad_gate, grad_up)
    ]
    return mixed, grads[1], grads[2], grads[0]


def solution(mesh):
    rows = P(("expert", "dp"), None)
    mats = P("expert", "dp", None)
    return jax.shard_map(
        body,
        mesh=mesh,
        in_specs=(rows, rows, rows, rows, mats, mats, mats),
        out_specs=(rows, mats, mats, mats),
        check_vma=False,
    )
```

profile of v0, /device:TPU:0, one launch (start us, length us, event | category | flops | bytes accessed | tf_op | source)
XLA Modules:
  0.0 221.2 jit_solution(8880502016269834853)
XLA Ops:
  7.2 0.7 all-gather.4.cloned.1.call-update
  8.0 0.7 all-gather.6.cloned.1.call-update
  8.8 0.6 pad_maximum_fusion.2.x_ref
  9.4 11.1 %shard_map.102 = f32[16,8,128]{2,1,0:T(8,128)} custom-call(f32[8,128]{1,0:T(8,128)} %pad_maximum_fusion.2.x_ref), custom_call_target="tpu_custom_call" | custom-call | tf_op jit(solution)/shard_map/pallas_call | solution.py:55
  20.5 1.2 collective-permute-start
  21.7 2.7 %collective-permute-start.2 = (bf16[128,1440]{0,1:T(8,128)(2,1)S(1)}, bf16[128,1440]{0,1:T(8,128)(2,1)S(1)}, u32[]{:S(2)}, u32[]{:S(2)}) collective-permute-start(bf16[128,1440]{0,1:T(8,128)(2,1)S(1)} %copy-done.1), channel_id=1, source_target_pairs={{0,24},{2,26},{4,28},{6,30},{8,0},{10,2},{12,4},{14,6},{16,8},{18,... | collective-permute-start | bytes 1105928 | tf_op jit(solution)/shard_map/ppermute | solution.py:82
  24.5 0.6 fusion.61
  27.7 1.0 select_reduce_fusion.1
  29.4 0.3 select_reduce_fusion.4
  29.8 0.5 broadcast_and_fusion
  30.5 1.2 copy.23
  31.9 1.9 collective-permute-done
  33.8 3.0 %collective-permute-start.1 = (bf16[128,1440]{0,1:T(8,128)(2,1)S(1)}, bf16[128,1440]{0,1:T(8,128)(2,1)S(1)}, u32[]{:S(2)}, u32[]{:S(2)}) collective-permute-start(bf16[128,1440]{0,1:T(8,128)(2,1)S(1)} %collective-permute-done), channel_id=1, source_target_pairs={{0,8},{2,10},{4,12},{6,14},{8,16},{10,18},{12,20},{14,22},{16,24},... | collective-permute-start | bytes 1105928 | tf_op jit(solution)/shard_map/ppermute | solution.py:82
  36.7 0.5 select_reduce_fusion
  37.2 0.4 fusion.60
  37.6 2.0 collective-permute-done.2
  39.7 8.0 %collective-permute-done.1 = bf16[128,1440]{0,1:T(8,128)(2,1)S(1)} collective-permute-done((bf16[128,1440]{0,1:T(8,128)(2,1)S(1)}, bf16[128,1440]{0,1:T(8,128)(2,1)S(1)}, u32[]{:S(2)}, u32[]{:S(2)}) %collective-permute-start.1) | collective-permute-done | bytes 368672 | tf_op jit(solution)/shard_map/ppermute | solution.py:82
  47.6 3.8 %collective-permute-start.8 = (bf16[128,1440]{0,1:T(8,128)(2,1)S(1)}, bf16[128,1440]{0,1:T(8,128)(2,1)S(1)}, u32[]{:S(2)}, u32[]{:S(2)}) collective-permute-start(bf16[128,1440]{0,1:T(8,128)(2,1)S(1)} %copy-done.2), channel_id=1, source_target_pairs={{0,24},{2,26},{4,28},{6,30},{8,0},{10,2},{12,4},{14,6},{16,8},{18,... | collective-permute-start | bytes 1105928 | tf_op jit(solution)/shard_map/ppermute | solution.py:82
  51.8 0.6 convolution_convert_fusion.11
  52.5 1.6 collective-permute-start.3
  54.0 0.6 convolution_convert_fusion.10
  54.7 1.5 collective-permute-start.4
  56.2 0.6 convolution_convert_fusion.9
  56.8 0.6 collective-permute-start.5
  57.4 0.6 convolution_convert_fusion.12
  58.1 2.8 %collective-permute-done.6 = bf16[128,1440]{0,1:T(8,128)(2,1)S(1)} collective-permute-done((bf16[128,1440]{0,1:T(8,128)(2,1)S(1)}, bf16[128,1440]{0,1:T(8,128)(2,1)S(1)}, u32[]{:S(2)}, u32[]{:S(2)}) %collective-permute-start.6) | collective-permute-done | bytes 368672 | tf_op jit(solution)/shard_map/ppermute | solution.py:82
  61.1 12.5 %collective-permute-done.7 = bf16[128,1440]{0,1:T(8,128)(2,1)S(1)} collective-permute-done((bf16[128,1440]{0,1:T(8,128)(2,1)S(1)}, bf16[128,1440]{0,1:T(8,128)(2,1)S(1)}, u32[]{:S(2)}, u32[]{:S(2)}) %collective-permute-start.7) | collective-permute-done | bytes 368672 | tf_op jit(solution)/shard_map/ppermute | solution.py:82
  73.8 0.6 convolution_convert_fusion.6
  74.4 1.9 collective-permute-start.10
  76.3 0.6 convolution_convert_fusion.5
  77.0 1.5 collective-permute-start.11
  78.5 0.6 convolution_convert_fusion.7
  79.2 0.2 collective-permute-start.9
  79.4 14.0 %collective-permute-done.4 = bf16[192,1440]{1,0:T(8,128)(2,1)S(1)} collective-permute-done((bf16[192,1440]{1,0:T(8,128)(2,1)S(1)}, bf16[192,1440]{1,0:T(8,128)(2,1)S(1)}, u32[]{:S(2)}, u32[]{:S(2)}) %collective-permute-start.4) | collective-permute-done | bytes 552992 | tf_op jit(solution)/shard_map/ppermute | solution.py:97
  93.3 2.5 %convolution_convert_fusion.4 = bf16[512,1440]{0,1:T(8,128)(2,1)} fusion(bf16[192,1440]{1,0:T(8,128)(2,1)S(1)} %collective-permute-done.5, bf16[192,1440]{1,0:T(8,128)(2,1)S(1)} %collective-permute-done.4, bf16[192,1440]{1,0:T(8,128)(2,1)S(1)} %collective-permute-done.3, bf16[192,1440]{1,0:T(8,128)(2,1)S(1)} %convolution_convert_fusion.12, ...), kind=kOutput, calls=%fused_computation.19 | convolution fusion | flops 1142439936 | bytes 3689472 | tf_op jit(solution)/shard_map/dot_general | solution.py:18
  95.8 0.6 convolution_convert_fusion.8
  96.5 8.7 %collective-permute-done.10 = bf16[192,1440]{1,0:T(8,128)(2,1)S(1)} collective-permute-done((bf16[192,1440]{1,0:T(8,128)(2,1)S(1)}, bf16[192,1440]{1,0:T(8,128)(2,1)S(1)}, u32[]{:S(2)}, u32[]{:S(2)}) %collective-permute-start.10) | collective-permute-done | bytes 552992 | tf_op jit(solution)/shard_map/ppermute | solution.py:97
  105.2 1.6 pad_maximum_fusion
  106.8 6.3 %fusion.6 = f32[512,1440]{0,1:T(8,128)} fusion(bf16[512,1440]{0,1:T(8,128)(2,1)S(1)} %copy-done.6, bf16[1,1440,1440]{2,1,0:T(8,128)(2,1)} %all-gather.4.cloned.1.call-done), kind=kOutput, calls=%fused_computation.9 | convolution fusion | flops 2123366400 | bytes 8570880 | tf_op jit(solution)/shard_map/dot_general | solution.py:18
  113.2 8.4 %multiply_convert_fusion.2 = (bf16[512,1440]{0,1:T(8,128)(2,1)}, f32[512,1440]{0,1:T(8,128)}) fusion(f32[512,1440]{0,1:T(8,128)} %fusion.6, bf16[512,1440]{0,1:T(8,128)(2,1)S(1)} %copy-done.6, bf16[1,1440,1440]{2,1,0:T(8,128)(2,1)} %all-gather.6.cloned.1.call-done), kind=kOutput, calls=%fused_computation.22 | convolution fusion | flops 2129264640 | bytes 12994560 | tf_op jit(solution)/shard_map/dot_general | solution.py:18
  121.6 7.9 %convolution_convert_fusion.3 = bf16[768,1440]{0,1:T(8,128)(2,1)} fusion(s32[768]{0:T(1024)S(1)} %select_n.84, bf16[512,1440]{0,1:T(8,128)(2,1)} %get-tuple-element.61, bf16[1,1440,1440]{2,1,0:T(8,128)(2,1)} %all-gather.8.cloned.1.call-done, f32[512]{0:T(512)S(1)} %select_reduce_fusion), kind=kOutput, calls=%fused_computation.15 | convolution fusion | flops 3258802176 | bytes 7838720 | tf_op jit(solution)/shard_map/dot_general | solution.py:26
  129.5 2.8 %copy.19 = bf16[768,1440]{1,0:T(8,128)(2,1)S(1)} copy(bf16[768,1440]{0,1:T(8,128)(2,1)} %convolution_convert_fusion.3) | data formatting | bytes 4423680 | tf_op jit(solution)/shard_map/convert_element_type | solution.py:168
  132.3 3.2 %fusion.14 = bf16[512,1440]{0,1:T(8,128)(2,1)S(1)} fusion(bf16[768,1440]{1,0:T(8,128)(2,1)} %pad_maximum_fusion, f32[512]{0:T(512)S(1)} %select_reduce_fusion, s32[768]{0:T(1024)S(1)} %select_n.84), kind=kOutput, calls=%fused_computation.17 | convolution fusion | flops 1134329856 | bytes 3691520 | tf_op jit(solution)/shard_map/dot_general | solution.py:18
  135.5 1.3 slice_bitcast_fusion.3
  136.8 0.3 collective-permute-start.12
  137.1 1.7 collective-permute-start.13
  138.8 1.5 collective-permute-start.14
  140.3 7.8 %multiply_convert_fusion = (bf16[512,1440]{0,1:T(8,128)(2,1)}, bf16[512,1440]{0,1:T(8,128)(2,1)}) fusion(f32[512,1440]{0,1:T(8,128)S(1)} %copy-done.5, f32[512,1440]{0,1:T(8,128)S(1)} %copy-done.10, bf16[512,1440]{0,1:T(8,128)(2,1)S(1)} %fusion.14, bf16[1,1440,1440]{2,1,0:T(8,128)(2,1)} %all-gather.8.cloned.1.call-done), kind=kOutput, calls=%fused_computation.20 | convolution fusion | flops 2133688320 | bytes 14469120 | tf_op jit(solution)/shard_map/dot_general | solution.py:18
  148.0 4.6 %convolution_convert_fusion.2 = bf16[1440,1440]{1,0:T(8,128)(2,1)} fusion(bf16[512,1440]{0,1:T(8,128)(2,1)S(1)} %fusion.14, bf16[512,1440]{0,1:T(8,128)(2,1)S(1)} %copy-done.8), kind=kOutput, calls=%fused_computation.2 | convolution fusion | flops 2125440000 | bytes 7096320 | tf_op jit(solution)/shard_map/dot_general | solution.py:26
  152.6 0.6 collective-permute-done.12
  153.2 11.7 %collective-permute-done.13 = bf16[192,1440]{1,0:T(8,128)(2,1)S(1)} collective-permute-done((bf16[192,1440]{1,0:T(8,128)(2,1)}, bf16[192,1440]{1,0:T(8,128)(2,1)S(1)}, u32[]{:S(2)}, u32[]{:S(2)}) %collective-permute-start.13) | collective-permute-done | bytes 552992 | tf_op jit(solution)/shard_map/ppermute | solution.py:97
  164.9 0.2 pad_maximum_fusion.1
  165.1 0.8 copy-done
  165.9 1.4 fusion.26
  167.3 0.4 copy-done.9
  167.8 4.7 %convolution_convert_fusion = bf16[1440,1440]{1,0:T(8,128)(2,1)} fusion(bf16[512,1440]{0,1:T(8,128)(2,1)S(1)} %copy-done.7, bf16[512,1440]{0,1:T(8,128)(2,1)S(1)} %copy-done.9), kind=kOutput, calls=%fused_computation | convolution fusion | flops 2125440000 | bytes 7096320 | tf_op jit(solution)/shard_map/dot_general | solution.py:26
  172.4 0.3 reduce-scatter.4.cloned.1.call-start
  172.7 6.9 %convolution_convert_fusion.1 = bf16[1440,1440]{1,0:T(8,128)(2,1)} fusion(bf16[512,1440]{0,1:T(8,128)(2,1)} %convolution_convert_fusion.4, bf16[512,1440]{0,1:T(8,128)(2,1)} %get-tuple-element.33), kind=kOutput, calls=%fused_computation.1 | convolution fusion | flops 2125440000 | bytes 7096320 | tf_op jit(solution)/shard_map/dot_general | solution.py:26
  179.7 0.5 reduce-scatter.8.cloned.1.call-update
  180.6 2.0 collective-permute-start.17
  182.6 16.1 %collective-permute-done.15 = bf16[128,1440]{0,1:T(8,128)(2,1)S(1)} collective-permute-done((bf16[128,1440]{0,1:T(8,128)(2,1)S(1)}, bf16[128,1440]{0,1:T(8,128)(2,1)S(1)}, u32[]{:S(2)}, u32[]{:S(2)}) %collective-permute-start.15) | collective-permute-done | bytes 368672 | tf_op jit(solution)/shard_map/ppermute | solution.py:82
  198.9 7.5 %collective-permute-done.16 = bf16[128,1440]{0,1:T(8,128)(2,1)S(1)} collective-permute-done((bf16[128,1440]{0,1:T(8,128)(2,1)S(1)}, bf16[128,1440]{0,1:T(8,128)(2,1)S(1)}, u32[]{:S(2)}, u32[]{:S(2)}) %collective-permute-start.16) | collective-permute-done | bytes 368672 | tf_op jit(solution)/shard_map/ppermute | solution.py:82
  206.4 0.9 fusion.39
  207.3 7.1 %reduce-scatter.8.cloned.1.call-done = bf16[720,1440]{1,0:T(8,128)(2,1)} async-done(((bf16[1440,1440]{1,0:T(8,128)(2,1)}), bf16[720,1440]{1,0:T(8,128)(2,1)}) %reduce-scatter.8.cloned.1.call-update) | async-done | bytes 2073616 | tf_op jit(solution)/shard_map/reduce_scatter | solution.py:205
  (72 shorter events, 2.6 us)
Async XLA Ops:
  7.2 1.6 copy-start.3
  7.2 1.6 copy-start.4
  7.2 13.3 %copy-start.1 = (bf16[128,1440]{0,1:T(8,128)(2,1)S(1)}, bf16[128,1440]{0,1:T(8,128)(2,1)}, u32[]{:S(2)}) copy-start(bf16[128,1440]{0,1:T(8,128)(2,1)} %param.7) | copy-start | bytes 1105924
  7.2 99.6 %all-gather.4.cloned.1.call-start = ((), (), s32[]{:S(2)}) async-start(), calls=%async_computation.3 | async-start | bytes 6635520 | tf_op jit(solution)/shard_map/all_gather | solution.py:154
  7.9 105.3 %all-gather.6.cloned.1.call-start = ((), (), s32[]{:S(2)}) async-start(), calls=%async_computation.4 | async-start | bytes 6635520 | tf_op jit(solution)/shard_map/all_gather | solution.py:155
  8.7 112.9 %all-gather.8.cloned.1.call-start = ((), (), s32[]{:S(2)}) async-start(), calls=%async_computation.5 | async-start | bytes 6635520 | tf_op jit(solution)/shard_map/all_gather | solution.py:156
  20.5 27.2 %copy-start.2 = (bf16[128,1440]{0,1:T(8,128)(2,1)S(1)}, bf16[128,1440]{0,1:T(8,128)(2,1)}, u32[]{:S(2)}) copy-start(bf16[128,1440]{0,1:T(8,128)(2,1)} %param.8) | copy-start | bytes 1105924
  20.5 13.3 %collective-permute-start = (bf16[128,1440]{0,1:T(8,128)(2,1)S(1)}, bf16[128,1440]{0,1:T(8,128)(2,1)S(1)}, u32[]{:S(2)}, u32[]{:S(2)}) collective-permute-start(bf16[128,1440]{0,1:T(8,128)(2,1)S(1)} %copy-done.1), channel_id=1, source_target_pairs={{0,8},{2,10},{4,12},{6,14},{8,16},{10,18},{12,20},{14,22},{16,24},... | collective-permute-start | bytes 1105928 | tf_op jit(solution)/shard_map/ppermute | solution.py:82
  21.7 18.0 %collective-permute-start.2 = (bf16[128,1440]{0,1:T(8,128)(2,1)S(1)}, bf16[128,1440]{0,1:T(8,128)(2,1)S(1)}, u32[]{:S(2)}, u32[]{:S(2)}) collective-permute-start(bf16[128,1440]{0,1:T(8,128)(2,1)S(1)} %copy-done.1), channel_id=1, source_target_pairs={{0,24},{2,26},{4,28},{6,30},{8,0},{10,2},{12,4},{14,6},{16,8},{18,... | collective-permute-start | bytes 1105928 | tf_op jit(solution)/shard_map/ppermute | solution.py:82
  24.4 182.9 %reduce-scatter.6.cloned.1.call-start = ((), (), s32[]{:S(2)}) async-start(), calls=%async_computation.7 | async-start | bytes 6635520 | tf_op jit(solution)/shard_map/reduce_scatter | solution.py:205
  33.8 13.9 %collective-permute-start.1 = (bf16[128,1440]{0,1:T(8,128)(2,1)S(1)}, bf16[128,1440]{0,1:T(8,128)(2,1)S(1)}, u32[]{:S(2)}, u32[]{:S(2)}) collective-permute-start(bf16[128,1440]{0,1:T(8,128)(2,1)S(1)} %collective-permute-done), channel_id=1, source_target_pairs={{0,8},{2,10},{4,12},{6,14},{8,16},{10,18},{12,20},{14,22},{16,24},... | collective-permute-start | bytes 1105928 | tf_op jit(solution)/shard_map/ppermute | solution.py:82
  47.6 13.3 %collective-permute-start.6 = (bf16[128,1440]{0,1:T(8,128)(2,1)S(1)}, bf16[128,1440]{0,1:T(8,128)(2,1)S(1)}, u32[]{:S(2)}, u32[]{:S(2)}) collective-permute-start(bf16[128,1440]{0,1:T(8,128)(2,1)S(1)} %copy-done.2), channel_id=1, source_target_pairs={{0,8},{2,10},{4,12},{6,14},{8,16},{10,18},{12,20},{14,22},{16,24},... | collective-permute-start | bytes 1105928 | tf_op jit(solution)/shard_map/ppermute | solution.py:82
  47.6 26.0 %collective-permute-start.8 = (bf16[128,1440]{0,1:T(8,128)(2,1)S(1)}, bf16[128,1440]{0,1:T(8,128)(2,1)S(1)}, u32[]{:S(2)}, u32[]{:S(2)}) collective-permute-start(bf16[128,1440]{0,1:T(8,128)(2,1)S(1)} %copy-done.2), channel_id=1, source_target_pairs={{0,24},{2,26},{4,28},{6,30},{8,0},{10,2},{12,4},{14,6},{16,8},{18,... | collective-permute-start | bytes 1105928 | tf_op jit(solution)/shard_map/ppermute | solution.py:82
  52.5 26.7 %collective-permute-start.3 = (bf16[192,1440]{1,0:T(8,128)(2,1)S(1)}, bf16[192,1440]{1,0:T(8,128)(2,1)S(1)}, u32[]{:S(2)}, u32[]{:S(2)}) collective-permute-start(bf16[192,1440]{1,0:T(8,128)(2,1)S(1)} %convolution_convert_fusion.11), channel_id=1, source_target_pairs={{0,2},{2,0},{4,6},{6,4},{8,10},{10,8},{12,14},{14,12},{16,18},{18,... | collective-permute-start | bytes 1658888 | tf_op jit(solution)/shard_map/ppermute | solution.py:97
  54.7 38.7 %collective-permute-start.4 = (bf16[192,1440]{1,0:T(8,128)(2,1)S(1)}, bf16[192,1440]{1,0:T(8,128)(2,1)S(1)}, u32[]{:S(2)}, u32[]{:S(2)}) collective-permute-start(bf16[192,1440]{1,0:T(8,128)(2,1)S(1)} %convolution_convert_fusion.10), channel_id=1, source_target_pairs={{0,4},{2,6},{4,0},{6,2},{8,12},{10,14},{12,8},{14,10},{16,20},{18,... | collective-permute-start | bytes 1658888 | tf_op jit(solution)/shard_map/ppermute | solution.py:97
  56.8 36.5 %collective-permute-start.5 = (bf16[192,1440]{1,0:T(8,128)(2,1)S(1)}, bf16[192,1440]{1,0:T(8,128)(2,1)S(1)}, u32[]{:S(2)}, u32[]{:S(2)}) collective-permute-start(bf16[192,1440]{1,0:T(8,128)(2,1)S(1)} %convolution_convert_fusion.9), channel_id=1, source_target_pairs={{0,6},{2,4},{4,2},{6,0},{8,14},{10,12},{12,10},{14,8},{16,22},{18,... | collective-permute-start | bytes 1658888 | tf_op jit(solution)/shard_map/ppermute | solution.py:97
  60.9 12.7 %collective-permute-start.7 = (bf16[128,1440]{0,1:T(8,128)(2,1)S(1)}, bf16[128,1440]{0,1:T(8,128)(2,1)S(1)}, u32[]{:S(2)}, u32[]{:S(2)}) collective-permute-start(bf16[128,1440]{0,1:T(8,128)(2,1)S(1)} %collective-permute-done.6), channel_id=1, source_target_pairs={{0,8},{2,10},{4,12},{6,14},{8,16},{10,18},{12,20},{14,22},{16,24},... | collective-permute-start | bytes 1105928 | tf_op jit(solution)/shard_map/ppermute | solution.py:82
  74.4 30.8 %collective-permute-start.10 = (bf16[192,1440]{1,0:T(8,128)(2,1)S(1)}, bf16[192,1440]{1,0:T(8,128)(2,1)S(1)}, u32[]{:S(2)}, u32[]{:S(2)}) collective-permute-start(bf16[192,1440]{1,0:T(8,128)(2,1)S(1)} %convolution_convert_fusion.6), channel_id=1, source_target_pairs={{0,4},{2,6},{4,0},{6,2},{8,12},{10,14},{12,8},{14,10},{16,20},{18,... | collective-permute-start | bytes 1658888 | tf_op jit(solution)/shard_map/ppermute | solution.py:97
  77.0 28.2 %collective-permute-start.11 = (bf16[192,1440]{1,0:T(8,128)(2,1)S(1)}, bf16[192,1440]{1,0:T(8,128)(2,1)S(1)}, u32[]{:S(2)}, u32[]{:S(2)}) collective-permute-start(bf16[192,1440]{1,0:T(8,128)(2,1)S(1)} %convolution_convert_fusion.5), channel_id=1, source_target_pairs={{0,6},{2,4},{4,2},{6,0},{8,14},{10,12},{12,10},{14,8},{16,22},{18,... | collective-permute-start | bytes 1658888 | tf_op jit(solution)/shard_map/ppermute | solution.py:97
  79.2 26.0 %collective-permute-start.9 = (bf16[192,1440]{1,0:T(8,128)(2,1)S(1)}, bf16[192,1440]{1,0:T(8,128)(2,1)S(1)}, u32[]{:S(2)}, u32[]{:S(2)}) collective-permute-start(bf16[192,1440]{1,0:T(8,128)(2,1)S(1)} %convolution_convert_fusion.7), channel_id=1, source_target_pairs={{0,2},{2,0},{4,6},{6,4},{8,10},{10,8},{12,14},{14,12},{16,18},{18,... | collective-permute-start | bytes 1658888 | tf_op jit(solution)/shard_map/ppermute | solution.py:97
  96.5 10.4 %copy-start.6 = (bf16[512,1440]{0,1:T(8,128)(2,1)S(1)}, bf16[512,1440]{0,1:T(8,128)(2,1)}, u32[]{:S(2)}) copy-start(bf16[512,1440]{0,1:T(8,128)(2,1)} %convolution_convert_fusion.4) | copy-start | bytes 4423684
  132.3 8.0 %copy-start.10 = (f32[512,1440]{0,1:T(8,128)S(1)}, f32[512,1440]{0,1:T(8,128)}, u32[]{:S(2)}) copy-start(f32[512,1440]{0,1:T(8,128)} %get-tuple-element.62) | copy-start | bytes 8847364
  135.5 4.8 %copy-start.5 = (f32[512,1440]{0,1:T(8,128)S(1)}, f32[512,1440]{0,1:T(8,128)}, u32[]{:S(2)}) copy-start(f32[512,1440]{0,1:T(8,128)} %fusion.6) | copy-start | bytes 8847364
  136.8 16.4 %collective-permute-start.12 = (bf16[192,1440]{1,0:T(8,128)(2,1)}, bf16[192,1440]{1,0:T(8,128)(2,1)S(1)}, u32[]{:S(2)}, u32[]{:S(2)}) collective-permute-start(bf16[192,1440]{1,0:T(8,128)(2,1)} %get-tuple-element.45), channel_id=1, source_target_pairs={{0,2},{2,0},{4,6},{6,4},{8,10},{10,8},{12,14},{14,12},{16,18},{18,... | collective-permute-start | bytes 1658888 | tf_op jit(solution)/shard_map/ppermute | solution.py:97
  137.1 27.8 %collective-permute-start.13 = (bf16[192,1440]{1,0:T(8,128)(2,1)}, bf16[192,1440]{1,0:T(8,128)(2,1)S(1)}, u32[]{:S(2)}, u32[]{:S(2)}) collective-permute-start(bf16[192,1440]{1,0:T(8,128)(2,1)} %get-tuple-element.44), channel_id=1, source_target_pairs={{0,4},{2,6},{4,0},{6,2},{8,12},{10,14},{12,8},{14,10},{16,20},{18,... | collective-permute-start | bytes 1658888 | tf_op jit(solution)/shard_map/ppermute | solution.py:97
  138.8 26.1 %collective-permute-start.14 = (bf16[192,1440]{1,0:T(8,128)(2,1)S(1)}, bf16[192,1440]{1,0:T(8,128)(2,1)S(1)}, u32[]{:S(2)}, u32[]{:S(2)}) collective-permute-start(bf16[192,1440]{1,0:T(8,128)(2,1)S(1)} %get-tuple-element.43), channel_id=1, source_target_pairs={{0,6},{2,4},{4,2},{6,0},{8,14},{10,12},{12,10},{14,8},{16,22},{18,... | collective-permute-start | bytes 1658888 | tf_op jit(solution)/shard_map/ppermute | solution.py:97
  140.3 7.8 %copy-start.8 = (bf16[512,1440]{0,1:T(8,128)(2,1)S(1)}, bf16[512,1440]{0,1:T(8,128)(2,1)}, u32[]{:S(2)}) copy-start(bf16[512,1440]{0,1:T(8,128)(2,1)} %get-tuple-element.61) | copy-start | bytes 4423684
  164.9 1.0 copy-start
  165.9 1.4 copy-start.7
  165.9 1.8 copy-start.9
  172.4 34.8 %reduce-scatter.4.cloned.1.call-start = ((), (), s32[]{:S(2)}) async-start(), calls=%async_computation.6 | async-start | bytes 6635520 | tf_op jit(solution)/shard_map/reduce_scatter | solution.py:205
  179.7 34.7 %reduce-scatter.8.cloned.1.call-start = ((), (), s32[]{:S(2)}) async-start(), calls=%async_computation.8 | async-start | bytes 6635520 | tf_op jit(solution)/shard_map/reduce_scatter | solution.py:205
  180.5 18.2 %collective-permute-start.15 = (bf16[128,1440]{0,1:T(8,128)(2,1)S(1)}, bf16[128,1440]{0,1:T(8,128)(2,1)S(1)}, u32[]{:S(2)}, u32[]{:S(2)}) collective-permute-start(bf16[128,1440]{0,1:T(8,128)(2,1)S(1)} %get-tuple-element.46), channel_id=1, source_target_pairs={{0,24},{2,26},{4,28},{6,30},{8,0},{10,2},{12,4},{14,6},{16,8},{18,... | collective-permute-start | bytes 1105928 | tf_op jit(solution)/shard_map/ppermute | solution.py:82
  180.6 18.3 %collective-permute-start.17 = (bf16[128,1440]{0,1:T(8,128)(2,1)S(1)}, bf16[128,1440]{0,1:T(8,128)(2,1)S(1)}, u32[]{:S(2)}, u32[]{:S(2)}) collective-permute-start(bf16[128,1440]{0,1:T(8,128)(2,1)S(1)} %get-tuple-element.47), channel_id=1, source_target_pairs={{0,8},{2,10},{4,12},{6,14},{8,16},{10,18},{12,20},{14,22},{16,24},... | collective-permute-start | bytes 1105928 | tf_op jit(solution)/shard_map/ppermute | solution.py:82
  198.8 7.6 %collective-permute-start.16 = (bf16[128,1440]{0,1:T(8,128)(2,1)S(1)}, bf16[128,1440]{0,1:T(8,128)(2,1)S(1)}, u32[]{:S(2)}, u32[]{:S(2)}) collective-permute-start(bf16[128,1440]{0,1:T(8,128)(2,1)S(1)} %fusion.37), channel_id=1, source_target_pairs={{0,24},{2,26},{4,28},{6,30},{8,0},{10,2},{12,4},{14,6},{16,8},{18,... | collective-permute-start | bytes 1105928 | tf_op jit(solution)/shard_map/ppermute | solution.py:82
Sparse Core Ops, SparseCore 0:
  9.5 16.7 all-gather.3
  27.8 15.1 all-gather.5
  44.6 15.1 all-gather.7
  172.6 9.1 reduce-scatter.5
  184.5 13.5 reduce-scatter.3
  200.8 13.5 reduce-scatter.7
where the time goes:
time: 222 us; the launch traced here: 221 us
  waiting for transfers between devices  94.8 us (43%)
  matrix products  59 us (27%)
  starting transfers between devices  24.1 us (11%)
  between operations  17.1 us (8%)
  Pallas kernels  11.1 us (5%)
  local copies, waits for them, and re-layouts  8.56 us (4%)
  other arithmetic  6.46 us (3%)
    ppermute x9, waiting for transfers between devices, shift(): return lax.ppermute(x, 'expert', pairs)  50.8 us
    ppermute x9, waiting for transfers between devices, exchange(): moved[d] = lax.ppermute(blocks[d], 'expert', pairs)  35 us
    dot_general x15, matrix products, dot(): return jnp.dot(a, b, preferred_element_type=F32)  33.5 us
    dot_general x5, matrix products, dot_tn(): lax.dot_general(a, b, (((0,), (0,)), ((), ())), preferred_element_type=F32)  25.4 us
    ppermute x9, starting transfers between devices, shift(): return lax.ppermute(x, 'expert', pairs)  12.8 us
    pallas_call x1, Pallas kernels, share(): pl.pallas_call(functools.partial(share_kernel, size), out_shape=jax.Shape...  11.1 us
    ppermute x9, starting transfers between devices, exchange(): moved[d] = lax.ppermute(blocks[d], 'expert', pairs)  10.9 us
    reduce_scatter x3, waiting for transfers between devices, body(): lax.psum_scatter(g, 'dp', scatter_dimension=0, tiled=True)[None]  7.08 us
  transfers between devices with their start and end apart: 24, of which 12 were waited for; matrix products, arithmetic and copies ran while one was open for 23% of the time, Pallas kernels for 5%

commit v1 on v0

--- a/solution.py
+++ b/solution.py
@@ -6,6 +6,7 @@
 from jax.experimental import pallas as pl
 from jax.experimental.pallas import tpu as pltpu
 from jax.sharding import PartitionSpec as P
+
 
 CAP = 512
 INNER = 4
@@ -65,7 +66,7 @@
     )(x)
 
 
-def body(tokens, cotangent, expert_ids, gate_weights, w_gate, w_up, w_down):
+def layer(tokens, cotangent, expert_ids, gate_weights, w_gate, w_up, w_down):
     size = lax.axis_size("expert")
     rows, top = expert_ids.shape
     width = tokens.shape[1]
@@ -175,9 +176,7 @@
     d_hidden = dot(packed_g, full_down)
     d_gate = (d_hidden * (pre_up + 1.0) * slope).astype(BF16)
     d_up = (d_hidden * value).astype(BF16)
-    returned, grad_down, d_gate, d_up = lax.optimization_barrier(
-        (returned, grad_down, d_gate, d_up)
-    )
+    returned, d_gate, d_up = lax.optimization_barrier((returned, d_gate, d_up))
     partial = dot_tn(select.reshape(inner * outer * slot, outer * rows), returned)
     partial = partial.reshape(outer, rows, width)
     partial, d_gate, d_up = lax.optimization_barrier((partial, d_gate, d_up))
@@ -212,7 +211,7 @@
     rows = P(("expert", "dp"), None)
     mats = P("expert", "dp", None)
     return jax.shard_map(
-        body,
+        layer,
         mesh=mesh,
         in_specs=(rows, rows, rows, rows, mats, mats, mats),
         out_specs=(rows, mats, mats, mats),

time: 222 us -> 216 us (0.973)
  waiting for transfers between devices: 94.8 us -> 89.4 us
    reduce_scatter x3, waiting for transfers between devices: 7.08 us -> 0.01 us  [layer(): lax.psum_scatter(g, 'dp', scatter_dimension=0, tiled=True)[None]]
    ppermute x9, waiting for transfers between devices: 50.8 us -> 54.8 us  [shift(): return lax.ppermute(x, 'expert', pairs)]
  transfers between devices with their start and end apart: 24 -> 24, of which waited for: 12 -> 12; matrix products, arithmetic and copies ran while one was open for 23% -> 24% of each run, Pallas kernels for 5% -> 5%
where the time goes in v1:
time: 216 us; the launch traced here: 215 us
  waiting for transfers between devices  89.4 us (41%)
  matrix products  59.6 us (28%)
  starting transfers between devices  26 us (12%)
  between operations  17.2 us (8%)
  Pallas kernels  11.1 us (5%)
  local copies, waits for them, and re-layouts  6.65 us (3%)
  other arithmetic  5.58 us (3%)
    ppermute x9, waiting for transfers between devices, shift(): return lax.ppermute(x, 'expert', pairs)  54.8 us
    dot_general x15, matrix products, dot(): return jnp.dot(a, b, preferred_element_type=F32)  34.6 us
    ppermute x9, waiting for transfers between devices, exchange(): moved[d] = lax.ppermute(blocks[d], 'expert', pairs)  33.1 us
    dot_general x5, matrix products, dot_tn(): lax.dot_general(a, b, (((0,), (0,)), ((), ())), preferred_element_type=F32)  25 us
    ppermute x9, starting transfers between devices, shift(): return lax.ppermute(x, 'expert', pairs)  15 us
    pallas_call x1, Pallas kernels, share(): pl.pallas_call(functools.partial(share_kernel, size), out_shape=jax.Shape...  11.1 us
    ppermute x9, starting transfers between devices, exchange(): moved[d] = lax.ppermute(blocks[d], 'expert', pairs)  10.8 us
  transfers between devices with their start and end apart: 24, of which 12 were waited for; matrix products, arithmetic and copies ran while one was open for 24% of the time, Pallas kernels for 5%

profile of v1, /device:TPU:0, one launch (start us, length us, event | category | flops | bytes accessed | tf_op | source)
XLA Modules:
  0.0 215.4 jit_solution(14468110275879906204)
XLA Ops:
  7.2 0.7 all-gather.4.cloned.1.call-update
  8.0 0.7 all-gather.6.cloned.1.call-update
  8.8 0.6 pad_maximum_fusion.2.x_ref
  9.4 11.1 %shard_map.102 = f32[16,8,128]{2,1,0:T(8,128)} custom-call(f32[8,128]{1,0:T(8,128)} %pad_maximum_fusion.2.x_ref), custom_call_target="tpu_custom_call" | custom-call | tf_op jit(solution)/shard_map/pallas_call | solution.py:56
  20.5 3.3 %collective-permute-start.2 = (bf16[128,1440]{0,1:T(8,128)(2,1)S(1)}, bf16[128,1440]{0,1:T(8,128)(2,1)S(1)}, u32[]{:S(2)}, u32[]{:S(2)}) collective-permute-start(bf16[128,1440]{0,1:T(8,128)(2,1)S(1)} %copy-done), channel_id=1, source_target_pairs={{0,24},{2,26},{4,28},{6,30},{8,0},{10,2},{12,4},{14,6},{16,8},{18,... | collective-permute-start | bytes 1105928 | tf_op jit(solution)/shard_map/ppermute | solution.py:83
  23.9 0.6 fusion.61
  27.6 0.1 fusion.31
  27.9 0.3 select_reduce_fusion.4
  28.5 0.6 broadcast_and_fusion
  29.0 10.5 %collective-permute-done = bf16[128,1440]{0,1:T(8,128)(2,1)S(1)} collective-permute-done((bf16[128,1440]{0,1:T(8,128)(2,1)S(1)}, bf16[128,1440]{0,1:T(8,128)(2,1)S(1)}, u32[]{:S(2)}, u32[]{:S(2)}) %collective-permute-start) | collective-permute-done | bytes 368672 | tf_op jit(solution)/shard_map/ppermute | solution.py:83
  39.5 1.7 collective-permute-start.1
  41.2 0.5 select_reduce_fusion
  41.7 0.4 fusion.60
  42.1 8.6 %collective-permute-done.1 = bf16[128,1440]{0,1:T(8,128)(2,1)S(1)} collective-permute-done((bf16[128,1440]{0,1:T(8,128)(2,1)S(1)}, bf16[128,1440]{0,1:T(8,128)(2,1)S(1)}, u32[]{:S(2)}, u32[]{:S(2)}) %collective-permute-start.1) | collective-permute-done | bytes 368672 | tf_op jit(solution)/shard_map/ppermute | solution.py:83
  50.7 2.0 collective-permute-start.6
  53.0 0.6 convolution_convert_fusion.9
  53.7 0.6 convolution_convert_fusion.10
  54.3 0.6 convolution_convert_fusion.11
  55.0 1.0 collective-permute-start.3
  55.9 1.6 collective-permute-start.4
  57.6 1.0 collective-permute-start.5
  58.5 0.6 convolution_convert_fusion.12
  59.2 6.6 %collective-permute-done.6 = bf16[128,1440]{0,1:T(8,128)(2,1)S(1)} collective-permute-done((bf16[128,1440]{0,1:T(8,128)(2,1)S(1)}, bf16[128,1440]{0,1:T(8,128)(2,1)S(1)}, u32[]{:S(2)}, u32[]{:S(2)}) %collective-permute-start.6) | collective-permute-done | bytes 368672 | tf_op jit(solution)/shard_map/ppermute | solution.py:83
  65.8 0.2 collective-permute-start.7
  66.2 9.3 %collective-permute-done.7 = bf16[128,1440]{0,1:T(8,128)(2,1)S(1)} collective-permute-done((bf16[128,1440]{0,1:T(8,128)(2,1)S(1)}, bf16[128,1440]{0,1:T(8,128)(2,1)S(1)}, u32[]{:S(2)}, u32[]{:S(2)}) %collective-permute-start.7) | collective-permute-done | bytes 368672 | tf_op jit(solution)/shard_map/ppermute | solution.py:83
  75.6 0.6 convolution_convert_fusion.7
  76.3 0.9 collective-permute-start.9
  77.2 0.6 convolution_convert_fusion.6
  77.8 1.7 collective-permute-start.10
  79.5 0.6 convolution_convert_fusion.5
  80.1 1.2 collective-permute-start.11
  81.3 1.1 collective-permute-done.5
  82.4 2.5 %convolution_convert_fusion.4 = bf16[512,1440]{0,1:T(8,128)(2,1)} fusion(bf16[192,1440]{1,0:T(8,128)(2,1)S(1)} %collective-permute-done.5, bf16[192,1440]{1,0:T(8,128)(2,1)S(1)} %collective-permute-done.4, bf16[192,1440]{1,0:T(8,128)(2,1)S(1)} %collective-permute-done.3, bf16[192,1440]{1,0:T(8,128)(2,1)S(1)} %convolution_convert_fusion.12, ...), kind=kOutput, calls=%fused_computation.19 | convolution fusion | flops 1142439936 | bytes 3689472 | tf_op jit(solution)/shard_map/dot_general | solution.py:19
  84.9 0.6 convolution_convert_fusion.8
  85.5 9.3 %collective-permute-done.9 = bf16[192,1440]{1,0:T(8,128)(2,1)S(1)} collective-permute-done((bf16[192,1440]{1,0:T(8,128)(2,1)S(1)}, bf16[192,1440]{1,0:T(8,128)(2,1)S(1)}, u32[]{:S(2)}, u32[]{:S(2)}) %collective-permute-start.9) | collective-permute-done | bytes 552992 | tf_op jit(solution)/shard_map/ppermute | solution.py:98
  94.8 9.9 %collective-permute-done.10 = bf16[192,1440]{1,0:T(8,128)(2,1)S(1)} collective-permute-done((bf16[192,1440]{1,0:T(8,128)(2,1)S(1)}, bf16[192,1440]{1,0:T(8,128)(2,1)S(1)}, u32[]{:S(2)}, u32[]{:S(2)}) %collective-permute-start.10) | collective-permute-done | bytes 552992 | tf_op jit(solution)/shard_map/ppermute | solution.py:98
  104.7 1.6 pad_maximum_fusion
  106.4 6.3 %fusion.6 = f32[512,1440]{0,1:T(8,128)} fusion(bf16[512,1440]{0,1:T(8,128)(2,1)S(1)} %copy-done.8, bf16[1,1440,1440]{2,1,0:T(8,128)(2,1)} %all-gather.4.cloned.1.call-done), kind=kOutput, calls=%fused_computation.9 | convolution fusion | flops 2123366400 | bytes 8570880 | tf_op jit(solution)/shard_map/dot_general | solution.py:19
  112.7 8.3 %multiply_convert_fusion.2 = (bf16[512,1440]{0,1:T(8,128)(2,1)}, f32[512,1440]{0,1:T(8,128)}) fusion(f32[512,1440]{0,1:T(8,128)} %fusion.6, bf16[512,1440]{0,1:T(8,128)(2,1)S(1)} %copy-done.8, bf16[1,1440,1440]{2,1,0:T(8,128)(2,1)} %all-gather.6.cloned.1.call-done), kind=kOutput, calls=%fused_computation.22 | convolution fusion | flops 2129264640 | bytes 12994560 | tf_op jit(solution)/shard_map/dot_general | solution.py:19
  121.0 7.9 %convolution_convert_fusion.3 = bf16[768,1440]{0,1:T(8,128)(2,1)} fusion(s32[768]{0:T(1024)S(1)} %select_n.84, bf16[512,1440]{0,1:T(8,128)(2,1)} %get-tuple-element.59, bf16[1,1440,1440]{2,1,0:T(8,128)(2,1)} %all-gather.8.cloned.1.call-done, f32[512]{0:T(512)S(1)} %select_reduce_fusion), kind=kOutput, calls=%fused_computation.15 | convolution fusion | flops 3258802176 | bytes 7838720 | tf_op jit(solution)/shard_map/dot_general | solution.py:27
  128.9 2.8 %copy.19 = bf16[768,1440]{1,0:T(8,128)(2,1)S(1)} copy(bf16[768,1440]{0,1:T(8,128)(2,1)} %convolution_convert_fusion.3) | data formatting | bytes 4423680 | tf_op jit(solution)/shard_map/convert_element_type | solution.py:169
  131.8 3.2 %fusion.14 = bf16[512,1440]{0,1:T(8,128)(2,1)S(1)} fusion(bf16[768,1440]{1,0:T(8,128)(2,1)} %pad_maximum_fusion, f32[512]{0:T(512)S(1)} %select_reduce_fusion, s32[768]{0:T(1024)S(1)} %select_n.84), kind=kOutput, calls=%fused_computation.17 | convolution fusion | flops 1134329856 | bytes 3691520 | tf_op jit(solution)/shard_map/dot_general | solution.py:19
  134.9 1.2 copy-done.6
  136.1 4.6 %convolution_convert_fusion = bf16[1440,1440]{1,0:T(8,128)(2,1)} fusion(bf16[512,1440]{0,1:T(8,128)(2,1)S(1)} %fusion.14, bf16[512,1440]{0,1:T(8,128)(2,1)S(1)} %copy-done.10), kind=kOutput, calls=%fused_computation | convolution fusion | flops 2125440000 | bytes 7096320 | tf_op jit(solution)/shard_map/dot_general | solution.py:27
  140.8 0.2 copy.63
  141.0 0.5 copy.23
  141.5 0.2 slice_bitcast_fusion.3
  141.7 1.7 collective-permute-start.14
  143.4 1.3 collective-permute-start.13
  144.6 0.6 collective-permute-start.12
  145.2 8.9 %multiply_convert_fusion = (bf16[512,1440]{0,1:T(8,128)(2,1)}, bf16[512,1440]{0,1:T(8,128)(2,1)S(1)}) fusion(f32[512,1440]{0,1:T(8,128)S(1)} %copy-done.5, f32[512,1440]{0,1:T(8,128)} %get-tuple-element.60, bf16[512,1440]{0,1:T(8,128)(2,1)S(1)} %copy-done.7, bf16[1,1440,1440]{2,1,0:T(8,128)(2,1)} %all-gather.8.cloned.1.call-done), kind=kOutput, calls=%fused_computation.20 | convolution fusion | flops 2133688320 | bytes 14469120 | tf_op jit(solution)/shard_map/dot_general | solution.py:19
  154.2 4.7 %collective-permute-done.14 = bf16[192,1440]{1,0:T(8,128)(2,1)S(1)} collective-permute-done((bf16[192,1440]{1,0:T(8,128)(2,1)S(1)}, bf16[192,1440]{1,0:T(8,128)(2,1)S(1)}, u32[]{:S(2)}, u32[]{:S(2)}) %collective-permute-start.14) | collective-permute-done | bytes 552992 | tf_op jit(solution)/shard_map/ppermute | solution.py:98
  158.8 8.1 %collective-permute-done.13 = bf16[192,1440]{1,0:T(8,128)(2,1)S(1)} collective-permute-done((bf16[192,1440]{1,0:T(8,128)(2,1)S(1)}, bf16[192,1440]{1,0:T(8,128)(2,1)S(1)}, u32[]{:S(2)}, u32[]{:S(2)}) %collective-permute-start.13) | collective-permute-done | bytes 552992 | tf_op jit(solution)/shard_map/ppermute | solution.py:98
  167.0 0.2 pad_maximum_fusion.1
  167.2 1.4 fusion.26
  168.6 4.6 %convolution_convert_fusion.2 = bf16[1440,1440]{1,0:T(8,128)(2,1)} fusion(bf16[512,1440]{0,1:T(8,128)(2,1)S(1)} %copy-done.9, bf16[512,1440]{0,1:T(8,128)(2,1)S(1)} %get-tuple-element.32), kind=kOutput, calls=%fused_computation.2 | convolution fusion | flops 2125440000 | bytes 7096320 | tf_op jit(solution)/shard_map/dot_general | solution.py:27
  173.2 6.5 %convolution_convert_fusion.1 = bf16[1440,1440]{1,0:T(8,128)(2,1)} fusion(bf16[512,1440]{0,1:T(8,128)(2,1)} %convolution_convert_fusion.4, bf16[512,1440]{0,1:T(8,128)(2,1)} %get-tuple-element.33), kind=kOutput, calls=%fused_computation.1 | convolution fusion | flops 2125440000 | bytes 7096320 | tf_op jit(solution)/shard_map/dot_general | solution.py:27
  179.8 0.2 convert.4
  180.0 3.3 %collective-permute-start.15 = (bf16[128,1440]{0,1:T(8,128)(2,1)S(1)}, bf16[128,1440]{0,1:T(8,128)(2,1)S(1)}, u32[]{:S(2)}, u32[]{:S(2)}) collective-permute-start(bf16[128,1440]{0,1:T(8,128)(2,1)S(1)} %get-tuple-element.44), channel_id=1, source_target_pairs={{0,24},{2,26},{4,28},{6,30},{8,0},{10,2},{12,4},{14,6},{16,8},{18,... | collective-permute-start | bytes 1105928 | tf_op jit(solution)/shard_map/ppermute | solution.py:83
  183.4 9.0 %collective-permute-done.15 = bf16[128,1440]{0,1:T(8,128)(2,1)S(1)} collective-permute-done((bf16[128,1440]{0,1:T(8,128)(2,1)S(1)}, bf16[128,1440]{0,1:T(8,128)(2,1)S(1)}, u32[]{:S(2)}, u32[]{:S(2)}) %collective-permute-start.15) | collective-permute-done | bytes 368672 | tf_op jit(solution)/shard_map/ppermute | solution.py:83
  192.4 4.3 %collective-permute-start.16 = (bf16[128,1440]{0,1:T(8,128)(2,1)S(1)}, bf16[128,1440]{0,1:T(8,128)(2,1)S(1)}, u32[]{:S(2)}, u32[]{:S(2)}) collective-permute-start(bf16[128,1440]{0,1:T(8,128)(2,1)S(1)} %fusion.37), channel_id=1, source_target_pairs={{0,24},{2,26},{4,28},{6,30},{8,0},{10,2},{12,4},{14,6},{16,8},{18,... | collective-permute-start | bytes 1105928 | tf_op jit(solution)/shard_map/ppermute | solution.py:83
  196.8 4.0 %collective-permute-done.17 = bf16[128,1440]{0,1:T(8,128)(2,1)S(1)} collective-permute-done((bf16[128,1440]{0,1:T(8,128)(2,1)S(1)}, bf16[128,1440]{0,1:T(8,128)(2,1)S(1)}, u32[]{:S(2)}, u32[]{:S(2)}) %collective-permute-start.17) | collective-permute-done | bytes 368672 | tf_op jit(solution)/shard_map/ppermute | solution.py:83
  200.7 6.9 %collective-permute-done.16 = bf16[128,1440]{0,1:T(8,128)(2,1)S(1)} collective-permute-done((bf16[128,1440]{0,1:T(8,128)(2,1)S(1)}, bf16[128,1440]{0,1:T(8,128)(2,1)S(1)}, u32[]{:S(2)}, u32[]{:S(2)}) %collective-permute-start.16) | collective-permute-done | bytes 368672 | tf_op jit(solution)/shard_map/ppermute | solution.py:83
  207.7 0.9 fusion.39
  (72 shorter events, 2.0 us)
Async XLA Ops:
  7.2 1.6 copy-start.3
  7.2 1.6 copy-start.4
  7.2 13.3 %copy-start = (bf16[128,1440]{0,1:T(8,128)(2,1)S(1)}, bf16[128,1440]{0,1:T(8,128)(2,1)}, u32[]{:S(2)}) copy-start(bf16[128,1440]{0,1:T(8,128)(2,1)} %param.7) | copy-start | bytes 1105924
  7.2 99.2 %all-gather.4.cloned.1.call-start = ((), (), s32[]{:S(2)}) async-start(), calls=%async_computation.3 | async-start | bytes 6635520 | tf_op jit(solution)/shard_map/all_gather | solution.py:155
  7.9 104.8 %all-gather.6.cloned.1.call-start = ((), (), s32[]{:S(2)}) async-start(), calls=%async_computation.4 | async-start | bytes 6635520 | tf_op jit(solution)/shard_map/all_gather | solution.py:156
  8.7 42.0 %copy-start.1 = (bf16[128,1440]{0,1:T(8,128)(2,1)S(1)}, bf16[128,1440]{0,1:T(8,128)(2,1)}, u32[]{:S(2)}) copy-start(bf16[128,1440]{0,1:T(8,128)(2,1)} %param.8) | copy-start | bytes 1105924
  8.7 112.3 %all-gather.8.cloned.1.call-start = ((), (), s32[]{:S(2)}) async-start(), calls=%async_computation.5 | async-start | bytes 6635520 | tf_op jit(solution)/shard_map/all_gather | solution.py:157
  20.5 6.7 %copy-start.2 = (f32[16,8,128]{2,1,0:T(8,128)S(1)}, f32[16,8,128]{2,1,0:T(8,128)}, u32[]{:S(2)}) copy-start(f32[16,8,128]{2,1,0:T(8,128)} %shard_map.102) | copy-start | bytes 196612
  20.5 21.6 %collective-permute-start.2 = (bf16[128,1440]{0,1:T(8,128)(2,1)S(1)}, bf16[128,1440]{0,1:T(8,128)(2,1)S(1)}, u32[]{:S(2)}, u32[]{:S(2)}) collective-permute-start(bf16[128,1440]{0,1:T(8,128)(2,1)S(1)} %copy-done), channel_id=1, source_target_pairs={{0,24},{2,26},{4,28},{6,30},{8,0},{10,2},{12,4},{14,6},{16,8},{18,... | collective-permute-start | bytes 1105928 | tf_op jit(solution)/shard_map/ppermute | solution.py:83
  23.8 15.7 %collective-permute-start = (bf16[128,1440]{0,1:T(8,128)(2,1)S(1)}, bf16[128,1440]{0,1:T(8,128)(2,1)S(1)}, u32[]{:S(2)}, u32[]{:S(2)}) collective-permute-start(bf16[128,1440]{0,1:T(8,128)(2,1)S(1)} %copy-done), channel_id=1, source_target_pairs={{0,8},{2,10},{4,12},{6,14},{8,16},{10,18},{12,20},{14,22},{16,24},... | collective-permute-start | bytes 1105928 | tf_op jit(solution)/shard_map/ppermute | solution.py:83
  23.8 184.7 %reduce-scatter.8.cloned.1.call-start = ((), (), s32[]{:S(2)}) async-start(), calls=%async_computation.8 | async-start | bytes 6635520 | tf_op jit(solution)/shard_map/reduce_scatter | solution.py:204
  39.5 11.2 %collective-permute-start.1 = (bf16[128,1440]{0,1:T(8,128)(2,1)S(1)}, bf16[128,1440]{0,1:T(8,128)(2,1)S(1)}, u32[]{:S(2)}, u32[]{:S(2)}) collective-permute-start(bf16[128,1440]{0,1:T(8,128)(2,1)S(1)} %collective-permute-done), channel_id=1, source_target_pairs={{0,8},{2,10},{4,12},{6,14},{8,16},{10,18},{12,20},{14,22},{16,24},... | collective-permute-start | bytes 1105928 | tf_op jit(solution)/shard_map/ppermute | solution.py:83
  50.7 24.9 %collective-permute-start.8 = (bf16[128,1440]{0,1:T(8,128)(2,1)S(1)}, bf16[128,1440]{0,1:T(8,128)(2,1)S(1)}, u32[]{:S(2)}, u32[]{:S(2)}) collective-permute-start(bf16[128,1440]{0,1:T(8,128)(2,1)S(1)} %copy-done.1), channel_id=1, source_target_pairs={{0,24},{2,26},{4,28},{6,30},{8,0},{10,2},{12,4},{14,6},{16,8},{18,... | collective-permute-start | bytes 1105928 | tf_op jit(solution)/shard_map/ppermute | solution.py:83
  50.7 15.1 %collective-permute-start.6 = (bf16[128,1440]{0,1:T(8,128)(2,1)S(1)}, bf16[128,1440]{0,1:T(8,128)(2,1)S(1)}, u32[]{:S(2)}, u32[]{:S(2)}) collective-permute-start(bf16[128,1440]{0,1:T(8,128)(2,1)S(1)} %copy-done.1), channel_id=1, source_target_pairs={{0,8},{2,10},{4,12},{6,14},{8,16},{10,18},{12,20},{14,22},{16,24},... | collective-permute-start | bytes 1105928 | tf_op jit(solution)/shard_map/ppermute | solution.py:83
  55.0 25.1 %collective-permute-start.3 = (bf16[192,1440]{1,0:T(8,128)(2,1)S(1)}, bf16[192,1440]{1,0:T(8,128)(2,1)S(1)}, u32[]{:S(2)}, u32[]{:S(2)}) collective-permute-start(bf16[192,1440]{1,0:T(8,128)(2,1)S(1)} %convolution_convert_fusion.11), channel_id=1, source_target_pairs={{0,2},{2,0},{4,6},{6,4},{8,10},{10,8},{12,14},{14,12},{16,18},{18,... | collective-permute-start | bytes 1658888 | tf_op jit(solution)/shard_map/ppermute | solution.py:98
  55.9 25.3 %collective-permute-start.4 = (bf16[192,1440]{1,0:T(8,128)(2,1)S(1)}, bf16[192,1440]{1,0:T(8,128)(2,1)S(1)}, u32[]{:S(2)}, u32[]{:S(2)}) collective-permute-start(bf16[192,1440]{1,0:T(8,128)(2,1)S(1)} %convolution_convert_fusion.10), channel_id=1, source_target_pairs={{0,4},{2,6},{4,0},{6,2},{8,12},{10,14},{12,8},{14,10},{16,20},{18,... | collective-permute-start | bytes 1658888 | tf_op jit(solution)/shard_map/ppermute | solution.py:98
  57.6 24.8 %collective-permute-start.5 = (bf16[192,1440]{1,0:T(8,128)(2,1)S(1)}, bf16[192,1440]{1,0:T(8,128)(2,1)S(1)}, u32[]{:S(2)}, u32[]{:S(2)}) collective-permute-start(bf16[192,1440]{1,0:T(8,128)(2,1)S(1)} %convolution_convert_fusion.9), channel_id=1, source_target_pairs={{0,6},{2,4},{4,2},{6,0},{8,14},{10,12},{12,10},{14,8},{16,22},{18,... | collective-permute-start | bytes 1658888 | tf_op jit(solution)/shard_map/ppermute | solution.py:98
  65.8 9.7 %collective-permute-start.7 = (bf16[128,1440]{0,1:T(8,128)(2,1)S(1)}, bf16[128,1440]{0,1:T(8,128)(2,1)S(1)}, u32[]{:S(2)}, u32[]{:S(2)}) collective-permute-start(bf16[128,1440]{0,1:T(8,128)(2,1)S(1)} %collective-permute-done.6), channel_id=1, source_target_pairs={{0,8},{2,10},{4,12},{6,14},{8,16},{10,18},{12,20},{14,22},{16,24},... | collective-permute-start | bytes 1105928 | tf_op jit(solution)/shard_map/ppermute | solution.py:83
  76.3 18.6 %collective-permute-start.9 = (bf16[192,1440]{1,0:T(8,128)(2,1)S(1)}, bf16[192,1440]{1,0:T(8,128)(2,1)S(1)}, u32[]{:S(2)}, u32[]{:S(2)}) collective-permute-start(bf16[192,1440]{1,0:T(8,128)(2,1)S(1)} %convolution_convert_fusion.7), channel_id=1, source_target_pairs={{0,2},{2,0},{4,6},{6,4},{8,10},{10,8},{12,14},{14,12},{16,18},{18,... | collective-permute-start | bytes 1658888 | tf_op jit(solution)/shard_map/ppermute | solution.py:98
  77.8 26.9 %collective-permute-start.10 = (bf16[192,1440]{1,0:T(8,128)(2,1)S(1)}, bf16[192,1440]{1,0:T(8,128)(2,1)S(1)}, u32[]{:S(2)}, u32[]{:S(2)}) collective-permute-start(bf16[192,1440]{1,0:T(8,128)(2,1)S(1)} %convolution_convert_fusion.6), channel_id=1, source_target_pairs={{0,4},{2,6},{4,0},{6,2},{8,12},{10,14},{12,8},{14,10},{16,20},{18,... | collective-permute-start | bytes 1658888 | tf_op jit(solution)/shard_map/ppermute | solution.py:98
  80.1 24.6 %collective-permute-start.11 = (bf16[192,1440]{1,0:T(8,128)(2,1)S(1)}, bf16[192,1440]{1,0:T(8,128)(2,1)S(1)}, u32[]{:S(2)}, u32[]{:S(2)}) collective-permute-start(bf16[192,1440]{1,0:T(8,128)(2,1)S(1)} %convolution_convert_fusion.5), channel_id=1, source_target_pairs={{0,6},{2,4},{4,2},{6,0},{8,14},{10,12},{12,10},{14,8},{16,22},{18,... | collective-permute-start | bytes 1658888 | tf_op jit(solution)/shard_map/ppermute | solution.py:98
  85.5 20.8 %copy-start.8 = (bf16[512,1440]{0,1:T(8,128)(2,1)S(1)}, bf16[512,1440]{0,1:T(8,128)(2,1)}, u32[]{:S(2)}) copy-start(bf16[512,1440]{0,1:T(8,128)(2,1)} %convolution_convert_fusion.4) | copy-start | bytes 4423684
  131.7 4.4 %copy-start.10 = (bf16[512,1440]{0,1:T(8,128)(2,1)S(1)}, bf16[512,1440]{0,1:T(8,128)(2,1)}, u32[]{:S(2)}) copy-start(bf16[512,1440]{0,1:T(8,128)(2,1)} %get-tuple-element.59) | copy-start | bytes 4423684
  134.9 1.2 copy-start.6
  140.7 67.8 %reduce-scatter.4.cloned.1.call-start = ((), (), s32[]{:S(2)}) async-start(), calls=%async_computation.6 | async-start | bytes 6635520 | tf_op jit(solution)/shard_map/reduce_scatter | solution.py:204
  141.5 3.7 %copy-start.5 = (f32[512,1440]{0,1:T(8,128)S(1)}, f32[512,1440]{0,1:T(8,128)}, u32[]{:S(2)}) copy-start(f32[512,1440]{0,1:T(8,128)} %fusion.6) | copy-start | bytes 8847364
  141.5 3.7 %copy-start.7 = (bf16[512,1440]{0,1:T(8,128)(2,1)S(1)}, bf16[512,1440]{0,1:T(8,128)(2,1)}, u32[]{:S(2)}) copy-start(bf16[512,1440]{0,1:T(8,128)(2,1)} %copy-done.6) | copy-start | bytes 4423684
  141.7 17.2 %collective-permute-start.14 = (bf16[192,1440]{1,0:T(8,128)(2,1)S(1)}, bf16[192,1440]{1,0:T(8,128)(2,1)S(1)}, u32[]{:S(2)}, u32[]{:S(2)}) collective-permute-start(bf16[192,1440]{1,0:T(8,128)(2,1)S(1)} %get-tuple-element.41), channel_id=1, source_target_pairs={{0,6},{2,4},{4,2},{6,0},{8,14},{10,12},{12,10},{14,8},{16,22},{18,... | collective-permute-start | bytes 1658888 | tf_op jit(solution)/shard_map/ppermute | solution.py:98
  143.4 23.6 %collective-permute-start.13 = (bf16[192,1440]{1,0:T(8,128)(2,1)S(1)}, bf16[192,1440]{1,0:T(8,128)(2,1)S(1)}, u32[]{:S(2)}, u32[]{:S(2)}) collective-permute-start(bf16[192,1440]{1,0:T(8,128)(2,1)S(1)} %get-tuple-element.42), channel_id=1, source_target_pairs={{0,4},{2,6},{4,0},{6,2},{8,12},{10,14},{12,8},{14,10},{16,20},{18,... | collective-permute-start | bytes 1658888 | tf_op jit(solution)/shard_map/ppermute | solution.py:98
  144.6 22.3 %collective-permute-start.12 = (bf16[192,1440]{1,0:T(8,128)(2,1)S(1)}, bf16[192,1440]{1,0:T(8,128)(2,1)S(1)}, u32[]{:S(2)}, u32[]{:S(2)}) collective-permute-start(bf16[192,1440]{1,0:T(8,128)(2,1)S(1)} %get-tuple-element.43), channel_id=1, source_target_pairs={{0,2},{2,0},{4,6},{6,4},{8,10},{10,8},{12,14},{14,12},{16,18},{18,... | collective-permute-start | bytes 1658888 | tf_op jit(solution)/shard_map/ppermute | solution.py:98
  167.2 1.4 copy-start.9
  173.2 35.4 %reduce-scatter.6.cloned.1.call-start = ((), (), s32[]{:S(2)}) async-start(), calls=%async_computation.7 | async-start | bytes 6635520 | tf_op jit(solution)/shard_map/reduce_scatter | solution.py:204
  180.0 12.3 %collective-permute-start.15 = (bf16[128,1440]{0,1:T(8,128)(2,1)S(1)}, bf16[128,1440]{0,1:T(8,128)(2,1)S(1)}, u32[]{:S(2)}, u32[]{:S(2)}) collective-permute-start(bf16[128,1440]{0,1:T(8,128)(2,1)S(1)} %get-tuple-element.44), channel_id=1, source_target_pairs={{0,24},{2,26},{4,28},{6,30},{8,0},{10,2},{12,4},{14,6},{16,8},{18,... | collective-permute-start | bytes 1105928 | tf_op jit(solution)/shard_map/ppermute | solution.py:83
  183.4 17.4 %collective-permute-start.17 = (bf16[128,1440]{0,1:T(8,128)(2,1)S(1)}, bf16[128,1440]{0,1:T(8,128)(2,1)S(1)}, u32[]{:S(2)}, u32[]{:S(2)}) collective-permute-start(bf16[128,1440]{0,1:T(8,128)(2,1)S(1)} %get-tuple-element.45), channel_id=1, source_target_pairs={{0,8},{2,10},{4,12},{6,14},{8,16},{10,18},{12,20},{14,22},{16,24},... | collective-permute-start | bytes 1105928 | tf_op jit(solution)/shard_map/ppermute | solution.py:83
  192.4 15.3 %collective-permute-start.16 = (bf16[128,1440]{0,1:T(8,128)(2,1)S(1)}, bf16[128,1440]{0,1:T(8,128)(2,1)S(1)}, u32[]{:S(2)}, u32[]{:S(2)}) collective-permute-start(bf16[128,1440]{0,1:T(8,128)(2,1)S(1)} %fusion.37), channel_id=1, source_target_pairs={{0,24},{2,26},{4,28},{6,30},{8,0},{10,2},{12,4},{14,6},{16,8},{18,... | collective-permute-start | bytes 1105928 | tf_op jit(solution)/shard_map/ppermute | solution.py:83
Sparse Core Ops, SparseCore 0:
  9.5 16.7 all-gather.3
  27.8 15.2 all-gather.5
  44.6 15.1 all-gather.7
  140.9 11.7 reduce-scatter.7
  173.3 12.1 reduce-scatter.3
  188.3 13.5 reduce-scatter.5
